TPU v7x, 32 devices: a whole 2x2x4 slice. The times are simulated.
32 devices in a mesh: seq: 8 (over z, y), grp: 4 (over x, core).
Axes of the slice: x: 2, y: 2, z: 4, core: 2. Of those that a mesh axis runs over, the one named last changes fastest.
Arguments:
- frames: bfloat16 [16384, 1024], P(('seq', 'grp')), may hold values from -6 to 6
- ln1_gain: float32 [1024], replicated, may hold values from 0.1 to 1.9
- w_in: bfloat16 [1024, 2, 1024], P('seq', None, 'grp'), may hold values from -0.1875 to 0.1875
- w_dw: bfloat16 [31, 1024], replicated, may hold values from -1 to 1
- ln2_gain: float32 [1024], replicated, may hold values from 0.1 to 1.9
- ln2_bias: float32 [1024], replicated, may hold values from -3 to 3
- w_out: bfloat16 [1024, 1024], P('grp', 'seq'), may hold values from -0.1875 to 0.1875
- block_utt: int32 [128], replicated, may hold values from 0 to 31, as said below
- block_off: int32 [128], replicated, may hold values from 0 to 6, as said below
- lengths: int32 [32], replicated, may hold values from 1 to 896, as said below
Outputs:
- result: bfloat16 [16384, 1024], P(('seq', 'grp'))
Inputs may be any that keep to these rules, and one draw needn't show every extreme that they name: block_utt never falls along the blocks and names every utterance; each utterance is one run of 1 to 7 whole blocks, and some utterance has exactly 7. block_off counts the blocks of the run before a block, starting at 0. `lengths`: an utterance of n blocks has more than (n - 1) * 128 and at most n * 128 live frames.
All inputs are finite; a program needn't handle non-finite values.
Results may differ from a plain program's by a relative error of at most 0.0046.
Values may be sent and summed in bfloat16 or wider, within the bound.
A program may use at most 64 MiB of HBM per device.

v0:
```python
import jax
import jax.numpy as jnp
from jax import lax
from jax.sharding import PartitionSpec as P

D = 1024
KER = 31
BLK = 128


epsilon = 1e-05


def extended(block, sides, width):
    for axis, dim in sides:
        count = lax.axis_size(axis)
        forward = [(i, i + 1) for i in range(count - 1)]
        backward = [(target, source) for source, target in forward]
        low = lax.ppermute(
            lax.slice_in_dim(block, block.shape[dim] - width, None, axis=dim), axis, forward
        )
        high = lax.ppermute(lax.slice_in_dim(block, 0, width, axis=dim), axis, backward)
        block = jnp.concatenate([low, block, high], axis=dim)
    return block


def frame_keys(block_utt, block_off, lengths, first_row, row_count, margin):
    places = first_row - margin + jnp.arange(row_count + 2 * margin, dtype=jnp.int32)
    total_rows = block_utt.shape[0] * BLK
    inside = (places >= 0) & (places < total_rows)
    blocks = jnp.clip(places // BLK, 0, block_utt.shape[0] - 1)
    utterance = jnp.take(block_utt, blocks)
    position = jnp.take(block_off, blocks) * BLK + places % BLK
    living = inside & (position < jnp.take(lengths, utterance))
    return (jnp.where(living, utterance, -1), living[margin : margin + row_count])


def layer_norm(rows, gain):
    values = rows.astype(jnp.float32)
    average = jnp.mean(values, axis=1, keepdims=True)
    centered = values - average
    spread = jnp.mean(centered * centered, axis=1, keepdims=True)
    return (centered * lax.rsqrt(spread + epsilon) * gain).astype(jnp.bfloat16)


def gate_units(projected, living):
    half = projected.shape[1] // 2
    values = projected[:, :half] * jax.nn.sigmoid(projected[:, half:])
    return (values * living.astype(jnp.float32)[:, None]).astype(jnp.bfloat16)


def depthwise(widened, keys_wide, taps, row_count):
    margin = (taps.shape[0] - 1) // 2
    center = keys_wide[margin : margin + row_count]
    summed = jnp.zeros((row_count, widened.shape[1]), jnp.float32)
    for tap_index in range(taps.shape[0]):
        shifted = widened[tap_index : tap_index + row_count].astype(jnp.float32)
        same = (keys_wide[tap_index : tap_index + row_count] == center)[:, None]
        summed = summed + jnp.where(same, shifted, 0.0) * taps[tap_index].astype(jnp.float32)
    return summed


def finish(mixed, stat_sum, square_sum, width_total, gain, bias):
    average = stat_sum / width_total
    spread = square_sum / width_total - average * average
    normed = (mixed - average[:, None]) * lax.rsqrt(spread + epsilon)[:, None] * gain + bias
    return (normed * jax.nn.sigmoid(normed)).astype(jnp.bfloat16)


def project_rows(normed, row_count, column_count):

    def add_rows(total, weight_piece, start_row):
        piece_rows = weight_piece.shape[0]
        return jnp.dot(
            normed, weight_piece.reshape(piece_rows, -1), preferred_element_type=jnp.float32
        )

    return (add_rows, jnp.zeros((row_count, column_count), jnp.float32))


def per_device(
    frames, ln1_gain, w_in, w_dw, ln2_gain, ln2_bias, w_out, block_utt, block_off, lengths
):
    row_count = frames.shape[0]
    margin = (KER - 1) // 2
    own_first = lax.axis_index(("seq", "grp")) * row_count
    keys_wide, living = frame_keys(block_utt, block_off, lengths, own_first, row_count, margin)
    normed = layer_norm(frames, ln1_gain)
    w_in_rows, w_out_rows = (
        lax.all_gather(w_in, "grp", axis=2, tiled=True),
        lax.all_gather(w_out, "grp", axis=0, tiled=True),
    )
    add_rows, empty = project_rows(normed, row_count, 2 * D)
    projected = add_rows(empty, lax.all_gather(w_in_rows, "seq", axis=0, tiled=True), jnp.int32(0))
    gated = gate_units(projected, living)
    widened = extended(gated, ((("seq", "grp"), 0),), margin)
    mixed = depthwise(widened, keys_wide, w_dw, row_count)
    act = finish(
        mixed, jnp.sum(mixed, axis=1), jnp.sum(mixed * mixed, axis=1), float(D), ln2_gain, ln2_bias
    )
    output = jnp.dot(
        act,
        lax.all_gather(w_out_rows, "seq", axis=1, tiled=True),
        preferred_element_type=jnp.float32,
    )
    alive = living.astype(jnp.float32)[:, None]
    return (frames.astype(jnp.float32) + output * alive).astype(jnp.bfloat16)


def solution(mesh):
    return jax.shard_map(
        per_device,
        mesh=mesh,
        in_specs=(
            P(("seq", "grp"), None),
            P(),
            P("seq", None, "grp"),
            P(),
            P(),
            P(),
            P("grp", "seq"),
            P(),
            P(),
            P(),
        ),
        out_specs=P(("seq", "grp"), None),
        check_vma=False,
    )
```

profile of v0, /device:TPU:0, one launch (start us, length us, event | category | flops | bytes accessed | tf_op | source)
XLA Modules:
  0.0 152.2 jit_solution(5140980709808963621)
XLA Ops:
  6.5 10.5 %all_gather.12 = bf16[128,2,1024]{2,1,0:T(2,128)(2,1)} all-gather(bf16[128,2,256]{2,1,0:T(2,128)(2,1)} %param.14), channel_id=1, replica_groups=mesh['seq'=8,'grp'=4] {'grp'}, dimensions={2}, use_global_device_ids=true | all-gather | bytes 655360 | tf_op jit(solution)/shard_map/all_gather | solution.py:90
  17.0 0.0 all-gather.3.cloned.1.call-update
  17.0 0.0 all-gather.5.cloned.1.call-start
  17.1 6.5 %all_gather.14 = bf16[1024,128]{1,0:T(8,128)(2,1)} all-gather(bf16[256,128]{1,0:T(8,128)(2,1)} %param.18), channel_id=1, replica_groups=mesh['seq'=8,'grp'=4] {'grp'}, dimensions={0}, use_global_device_ids=true | all-gather | bytes 327680 | tf_op jit(solution)/shard_map/all_gather | solution.py:91
  23.6 0.0 all-gather.5.cloned.1.call-update
  23.6 2.1 %fusion.67 = (s32[1]{0:T(128)}, s32[1]{0:T(128)}, s32[1]{0:T(128)}, s32[1]{0:T(128)}, s32[1]{0:T(128)}, /*index=5*/s32[1]{0:T(128)}, s32[1]{0:T(128)}, s32[1]{0:...) fusion(s32[32]{0:T(128)} %param.21), kind=kLoop, calls=%fused_computation.200 | loop fusion | bytes 152 | tf_op jit(solution)/shard_map/jit(_take)/gather | solution.py:34
  25.7 1.8 %fusion.68 = (s32[1]{0:T(128)}, s32[1]{0:T(128)}, s32[1]{0:T(128)}, s32[1]{0:T(128)}, s32[1]{0:T(128)}, /*index=5*/s32[1]{0:T(128)}, s32[1]{0:T(128)}, s32[1]{0:...) fusion(s32[32]{0:T(128)} %param.21), kind=kLoop, calls=%fused_computation.201 | loop fusion | bytes 104 | tf_op jit(solution)/shard_map/jit(_take)/gather | solution.py:34
  27.6 0.0 copy-start.1
  27.6 3.8 %gather_fusion = s32[542]{0:T(1024)S(1)} fusion(s32[128]{0:T(128)S(1)} %copy-done, s32[1024]{0:T(1024)S(1)} %pad_clamp_fusion), kind=kCustom, calls=%fused_computation.clone | custom fusion | bytes 6504 | tf_op jit(solution)/shard_map/jit(_take)/gather | solution.py:33
  31.4 0.0 copy-start.2
  31.4 3.8 %gather_fusion.1 = s32[542]{0:T(1024)S(1)} fusion(s32[128]{0:T(128)S(1)} %copy-done.1, s32[1024]{0:T(1024)S(1)} %pad_clamp_fusion), kind=kCustom, calls=%fused_computation.1.clone | custom fusion | bytes 6504 | tf_op jit(solution)/shard_map/jit(_take)/gather | solution.py:32
  35.3 20.1 %fusion.62 = (s32[542]{0:T(1024)S(1)}, pred[542]{0:T(1024)(128)(4,1)S(1)}) fusion(s32[542]{0:T(1024)S(1)} %gather_fusion.1, s32[]{:T(128)S(6)} %sub.32, s32[]{:T(128)} %bitcast.31, s32[]{:T(128)} %bitcast.30, s32[]{:T(128)} %bitcast.29, s32[]{:T(128)} %bitcast.28, s32[]{:T(128)} %bitcast.27, s32[]{:T(128)} %bitcast.26, s32[]{:T(128)} %bitcast.25, ...), kind=kLoop, calls=%fused_computation.161 | loop fusion | flops 57452 | bytes 7178 | tf_op jit(solution)/shard_map/jit(_where)/select_n | solution.py:35
  55.4 0.1 slice_compare_fusion.29
  55.5 0.1 slice_compare_fusion.28
  55.6 0.1 slice_compare_fusion.27
  55.7 0.1 slice_convert_fusion.30
  55.8 0.1 slice_convert_fusion.31
  55.9 0.2 convert_reduce_fusion
  56.1 0.4 fusion.2
  56.5 33.8 %all-gather.3.cloned.1.call-done = bf16[1024,2,1024]{2,1,0:T(2,128)(2,1)} async-done(((bf16[128,2,1024]{2,1,0:T(2,128)(2,1)}), bf16[1024,2,1024]{2,1,0:T(2,128)(2,1)}) %all-gather.3.cloned.1.call-update) | async-done | bytes 4194320 | tf_op jit(solution)/shard_map/all_gather | solution.py:94
  90.3 3.6 %copy.11 = bf16[128,8,2,1024]{3,1,2,0:T(8,128)(2,1)S(1)} copy(bf16[128,8,2,1024]{3,2,1,0:T(2,128)(2,1)} %bitcast.67) | data formatting | bytes 8388608
  94.0 2.5 %fusion.12 = f32[512,2048]{1,0:T(8,128)S(1)} fusion(bf16[1024,2048]{1,0:T(8,128)(2,1)S(1)} %bitcast.68, bf16[512,1024]{1,0:T(8,128)(2,1)S(1)} %copy-done.2, f32[1024]{0:T(1024)S(1)} %copy-done.4, f32[512]{0:T(512)S(1)} %add_rsqrt_fusion.1, f32[512]{0:T(512)S(1)} %broadcast_multiply_fusion.1), kind=kOutput, calls=%fused_computation.49 | convolution fusion | flops 2150105088 | bytes 9445376 | tf_op jit(solution)/shard_map/dot_general | solution.py:74
  96.5 0.6 fusion.11
  97.0 0.0 copy-start.5
  97.1 0.0 copy-start.6
  97.1 1.3 collective-permute-start
  98.4 1.5 collective-permute-start.1
  99.9 0.1 slice_compare_fusion.26
  99.9 3.3 %collective-permute-done.1 = bf16[15,1024]{1,0:T(8,128)(2,1)S(1)} collective-permute-done((bf16[15,1024]{1,0:T(8,128)(2,1)S(1)}, bf16[15,1024]{1,0:T(8,128)(2,1)S(1)}, u32[]{:S(2)}, u32[]{:S(2)}) %collective-permute-start.1) | collective-permute-done | bytes 30752 | tf_op jit(solution)/shard_map/ppermute | solution.py:22
  103.2 19.4 %fusion.64 = (f32[512]{0:T(512)S(1)}, f32[512]{0:T(512)S(1)}, f32[512,1024]{1,0:T(8,128)S(1)}) fusion(f32[1024]{0:T(1024)S(1)} %bitcast.98, bf16[15,1024]{1,0:T(8,128)(2,1)S(1)} %collective-permute-done.1, bf16[512,1024]{1,0:T(8,128)(2,1)S(1)} %fusion.11, pred[512]{0:T(512)(128)(4,1)S(1)} %get-tuple-element.73, f32[1024]{0:T(1024)S(1)} %bitcast.99, ...), kind=kLoop, calls=%fused_computation.198 | loop fusion | flops 112720896 | bytes 3353600 | tf_op jit(solution)/shard_map/reduce_sum | solution.py:99
  122.6 18.7 %all-gather.5.cloned.1.call-done = bf16[1024,1024]{1,0:T(8,128)(2,1)} async-done(((bf16[1024,128]{1,0:T(8,128)(2,1)}), bf16[1024,1024]{1,0:T(8,128)(2,1)}) %all-gather.5.cloned.1.call-update) | async-done | bytes 2097168 | tf_op jit(solution)/shard_map/all_gather | solution.py:103
  141.3 4.1 %fusion.5 = bf16[512,1024]{1,0:T(8,128)(2,1)} fusion(bf16[512,1024]{1,0:T(8,128)(2,1)S(1)} %copy-done.2, bf16[1024,1024]{1,0:T(8,128)(2,1)} %all-gather.5.cloned.1.call-done, f32[512,1024]{1,0:T(8,128)S(1)} %get-tuple-element.8, f32[1024]{0:T(1024)S(1)} %copy-done.5, f32[1024]{0:T(1024)S(1)} %copy-done.6, f32[512]{0:T(512)S(1)} %get-tuple-element.75, ...), kind=kOutput, calls=%fused_computation.38 | convolution fusion | flops 1080557568 | bytes 6305792 | tf_op jit(solution)/shard_map/dot_general | solution.py:101
  (19 shorter events, 0.1 us)
Async XLA Ops:
  6.5 21.1 %copy-start = (s32[128]{0:T(128)S(1)}, s32[128]{0:T(128)}, u32[]{:S(2)}) copy-start(s32[128]{0:T(128)} %param.20) | copy-start | bytes 1540
  6.5 83.8 %all-gather.3.cloned.1.call-start = ((), (), s32[]{:S(2)}) async-start(), calls=%async_computation | async-start | bytes 4718592 | tf_op jit(solution)/shard_map/all_gather | solution.py:94
  17.0 124.3 %all-gather.5.cloned.1.call-start = ((), (), s32[]{:S(2)}) async-start(), calls=%async_computation.1 | async-start | bytes 2359296 | tf_op jit(solution)/shard_map/all_gather | solution.py:103
  27.6 3.8 %copy-start.1 = (s32[128]{0:T(128)S(1)}, s32[128]{0:T(128)}, u32[]{:S(2)}) copy-start(s32[128]{0:T(128)} %param.19) | copy-start | bytes 1540
  31.4 24.2 %copy-start.3 = (bf16[31,1024]{1,0:T(8,128)(2,1)S(1)}, bf16[31,1024]{1,0:T(8,128)(2,1)}, u32[]{:S(2)}) copy-start(bf16[31,1024]{1,0:T(8,128)(2,1)} %param.15) | copy-start | bytes 190468
  31.4 24.4 %copy-start.2 = (bf16[512,1024]{1,0:T(8,128)(2,1)S(1)}, bf16[512,1024]{1,0:T(8,128)(2,1)}, u32[]{:S(2)}) copy-start(bf16[512,1024]{1,0:T(8,128)(2,1)} %param.12) | copy-start | bytes 3145732
  90.3 3.6 %copy-start.4 = (f32[1024]{0:T(1024)S(1)}, f32[1024]{0:T(1024)}, u32[]{:S(2)}) copy-start(f32[1024]{0:T(1024)} %param.13) | copy-start | bytes 12292
  97.0 44.3 %copy-start.5 = (f32[1024]{0:T(1024)S(1)}, f32[1024]{0:T(1024)}, u32[]{:S(2)}) copy-start(f32[1024]{0:T(1024)} %param.17) | copy-start | bytes 12292
  97.1 44.3 %copy-start.6 = (f32[1024]{0:T(1024)S(1)}, f32[1024]{0:T(1024)}, u32[]{:S(2)}) copy-start(f32[1024]{0:T(1024)} %param.16) | copy-start | bytes 12292
  97.1 2.9 %collective-permute-start = (bf16[15,1024]{1,0:T(8,128)(2,1)S(1)}, bf16[15,1024]{1,0:T(8,128)(2,1)S(1)}, u32[]{:S(2)}, u32[]{:S(2)}) collective-permute-start(bf16[15,1024]{1,0:T(8,128)(2,1)S(1)} %get-tuple-element.11), channel_id=1, source_target_pairs={{0,1},{1,2},{2,3},{3,4},{4,5},{5,6},{6,7},{7,8},{8,9},{9,10},{10,1... | collective-permute-start | bytes 92168 | tf_op jit(solution)/shard_map/ppermute | solution.py:19
  98.4 4.9 %collective-permute-start.1 = (bf16[15,1024]{1,0:T(8,128)(2,1)S(1)}, bf16[15,1024]{1,0:T(8,128)(2,1)S(1)}, u32[]{:S(2)}, u32[]{:S(2)}) collective-permute-start(bf16[15,1024]{1,0:T(8,128)(2,1)S(1)} %get-tuple-element.12), channel_id=1, source_target_pairs={{1,0},{2,1},{3,2},{4,3},{5,4},{6,5},{7,6},{8,7},{9,8},{10,9},{11,1... | collective-permute-start | bytes 92168 | tf_op jit(solution)/shard_map/ppermute | solution.py:22
Sparse Core Ops, SparseCore 0:
  17.2 73.1 all-gather.2
  92.4 48.8 all-gather.4
where the time goes:
time: 153 us; the launch traced here: 152 us
  waiting for transfers between devices  55.8 us (36%)
  other arithmetic  41.3 us (27%)
  blocking collectives  17 us (11%)
  local copies, waits for them, and re-layouts  15.2 us (10%)
  between operations  13.6 us (9%)
  matrix products  6.55 us (4%)
  starting transfers between devices  2.81 us (2%)
    all_gather x1, waiting for transfers between devices, per_device(): lax.all_gather(w_in_rows, 'seq', axis=0, tiled=True)  33.8 us
    select_n x1, other arithmetic, frame_keys(): return (jnp.where(living, utterance, -1), living[margin:margin + row_count])  20.1 us
    reduce_sum x1, other arithmetic, per_device(): jnp.sum(mixed, axis=1)  19.4 us
    all_gather x1, waiting for transfers between devices, per_device(): lax.all_gather(w_out_rows, 'seq', axis=1, tiled=True)  18.7 us
    all_gather x1, blocking collectives, per_device(): lax.all_gather(w_in, 'grp', axis=2, tiled=True)  10.5 us
    all_gather x1, blocking collectives, per_device(): lax.all_gather(w_out, 'grp', axis=0, tiled=True)  6.53 us
    dot_general x1, matrix products, per_device(): jnp.dot(act, lax.all_gather(w_out_rows, 'seq', axis=1, tiled=True), prefe...  4.06 us
    gather x2, local copies, waits for them, and re-layouts, frame_keys(): living = inside & (position < jnp.take(lengths, utterance))  3.9 us
  transfers between devices with their start and end apart: 4, of which 3 were waited for; matrix products, arithmetic and copies ran while one was open for 39% of the time, Pallas kernels for 0%

commit v1 on v0

--- a/solution.py
+++ b/solution.py
@@ -1,6 +1,10 @@
+import functools
+
 import jax
 import jax.numpy as jnp
 from jax import lax
+from jax.experimental import pallas as pl
+from jax.experimental.pallas import tpu as pltpu
 from jax.sharding import PartitionSpec as P
 
 D = 1024
@@ -107,9 +111,482 @@
     return (frames.astype(jnp.float32) + output * alive).astype(jnp.bfloat16)
 
 
+MESH = pl.DeviceIdType.MESH
+HALO = 16
+LANES = 128
+
+
+def fused_kernel(
+    nz,
+    frames_hbm,
+    wi_hbm,
+    wo_hbm,
+    gain1,
+    taps,
+    gain2,
+    bias2,
+    utts,
+    offs,
+    lens,
+    out_hbm,
+    WI,
+    WO,
+    FR,
+    HB,
+    NM,
+    GB,
+    MX,
+    TP,
+    ACT,
+    OUT,
+    ssem,
+    rsem,
+    hs,
+    hr,
+    lsem,
+    osem,
+):
+    rows, width = FR.shape
+    krows = wi_hbm.shape[0]
+    orows, ocols = wo_hbm.shape
+    nblk = rows // BLK
+    chunks = width // LANES
+    per_group = wi_hbm.shape[1] // (2 * LANES)
+    seq = lax.axis_index("seq")
+    grp = lax.axis_index("grp")
+    nseq = lax.axis_size("seq")
+    ngrp = lax.axis_size("grp")
+    z, y = seq // 2, seq % 2
+    x, c = grp // 2, grp % 2
+    index = seq * ngrp + grp
+    total = nseq * ngrp
+    after = (index + 1) % total
+    before = (index + total - 1) % total
+    px = (seq, (1 - x) * 2 + c)
+    py = (z * 2 + 1 - y, grp)
+    pp = (seq, x * 2 + 1 - c)
+    pn = (after // ngrp, after % ngrp)
+    pb = (before // ngrp, before % ngrp)
+    up = (jnp.minimum(z + 1, nz - 1) * 2 + y, grp)
+    down = (jnp.maximum(z - 1, 0) * 2 + y, grp)
+    has_up = z < nz - 1
+    has_down = z > 0
+
+    own_in = WI.at[grp, pl.ds(pl.multiple_of(seq * krows, krows), krows), :]
+    own_out = WO.at[
+        pl.ds(pl.multiple_of(grp * orows, orows), orows),
+        pl.ds(pl.multiple_of(seq * ocols, ocols), ocols),
+    ]
+    load_in = pltpu.make_async_copy(wi_hbm, own_in, lsem.at[0])
+    load_out = pltpu.make_async_copy(wo_hbm, own_out, lsem.at[1])
+    load_fr = pltpu.make_async_copy(frames_hbm, FR, lsem.at[2])
+    load_in.start()
+    load_fr.start()
+    load_out.start()
+
+    barrier = pltpu.get_barrier_semaphore()
+    for peer in (px, py, pp, pn, pb):
+        pl.semaphore_signal(barrier, inc=1, device_id=peer, device_id_type=MESH)
+
+    @pl.when(has_up)
+    def _():
+        pl.semaphore_signal(barrier, inc=1, device_id=up, device_id_type=MESH)
+
+    @pl.when(has_down)
+    def _():
+        pl.semaphore_signal(barrier, inc=1, device_id=down, device_id_type=MESH)
+
+    load_in.wait()
+    pl.semaphore_wait(barrier, 5 + has_up.astype(jnp.int32) + has_down.astype(jnp.int32))
+
+    def slot(w, sx, sy, sz, sc, half=None):
+        g = sx * 2 + sc
+        s = sz * 2 + sy
+        if w == 0:
+            count = krows if half is None else krows // 2
+            first = s * krows + (0 if half is None else half * count)
+            return WI.at[g, pl.ds(pl.multiple_of(first, count), count), :]
+        count = orows if half is None else orows // 2
+        first = g * orows + (0 if half is None else half * count)
+        return WO.at[
+            pl.ds(pl.multiple_of(first, count), count),
+            pl.ds(pl.multiple_of(s * ocols, ocols), ocols),
+        ]
+
+    ZU, ZD = 0, nz - 1
+    XD, YD = 2 * nz - 2, 3 * nz - 2
+    XH, YH = 4 * nz - 2, 5 * nz - 2
+    PO, PY, PX, PXH, PYH = (6 * nz - 2 + i * nz for i in range(5))
+
+    def copy(w, ref, sem, dev):
+        return pltpu.make_async_remote_copy(
+            src_ref=ref,
+            dst_ref=ref,
+            send_sem=ssem.at[w, sem],
+            recv_sem=rsem.at[w, sem],
+            device_id=dev,
+            device_id_type=MESH,
+        )
+
+    def spread(w, sz):
+        ref = slot(w, x, y, sz, c)
+        copy(w, ref, XD + sz, px).start()
+        copy(w, ref, YD + sz, py).start()
+        copy(w, ref, PO + sz, pp).start()
+
+    def first_sends(w):
+        ref = slot(w, x, y, z, c)
+
+        @pl.when(has_up)
+        def _():
+            copy(w, ref, ZU, up).start()
+
+        @pl.when(has_down)
+        def _():
+            copy(w, ref, ZD, down).start()
+
+        spread(w, z)
+
+    def line(w, d):
+        @pl.when(z >= d)
+        def _():
+            ref = slot(w, x, y, z - d, c)
+            copy(w, ref, ZU + d - 1, down).wait_recv()
+            if d < nz - 1:
+
+                @pl.when(has_up)
+                def _():
+                    copy(w, ref, ZU + d, up).start()
+
+            spread(w, z - d)
+
+        @pl.when(z + d < nz)
+        def _():
+            ref = slot(w, x, y, z + d, c)
+            copy(w, ref, ZD + d - 1, up).wait_recv()
+            if d < nz - 1:
+
+                @pl.when(has_down)
+                def _():
+                    copy(w, ref, ZD + d, down).start()
+
+            spread(w, z + d)
+
+    def square_at(w, sz):
+        ref = slot(w, x, 1 - y, sz, c)
+        copy(w, ref, YD + sz, py).wait_recv()
+        copy(w, slot(w, x, 1 - y, sz, c, 0), XH + sz, px).start()
+        copy(w, ref, PY + sz, pp).start()
+        ref = slot(w, 1 - x, y, sz, c)
+        copy(w, ref, XD + sz, px).wait_recv()
+        copy(w, slot(w, 1 - x, y, sz, c, 1), YH + sz, py).start()
+        copy(w, ref, PX + sz, pp).start()
+
+    def corner_at(w, sz):
+        ref = slot(w, 1 - x, 1 - y, sz, c, 0)
+        copy(w, ref, XH + sz, px).wait_recv()
+        copy(w, ref, PXH + sz, pp).start()
+        ref = slot(w, 1 - x, 1 - y, sz, c, 1)
+        copy(w, ref, YH + sz, py).wait_recv()
+        copy(w, ref, PYH + sz, pp).start()
+
+    def at_distance(step, w, d):
+        if d == 0:
+            step(w, z)
+            return
+
+        @pl.when(z >= d)
+        def _():
+            step(w, z - d)
+
+        @pl.when(z + d < nz)
+        def _():
+            step(w, z + d)
+
+    def partner_near(w):
+        for sz in range(nz):
+            copy(w, slot(w, x, y, sz, 1 - c), PO + sz, pp).wait_recv()
+            copy(w, slot(w, x, 1 - y, sz, 1 - c), PY + sz, pp).wait_recv()
+
+    def partner_far(w):
+        for sz in range(nz):
+            copy(w, slot(w, 1 - x, y, sz, 1 - c), PX + sz, pp).wait_recv()
+            copy(w, slot(w, 1 - x, 1 - y, sz, 1 - c, 0), PXH + sz, pp).wait_recv()
+            copy(w, slot(w, 1 - x, 1 - y, sz, 1 - c, 1), PYH + sz, pp).wait_recv()
+
+    def halo_copy(src, dst, sem, dev):
+        return pltpu.make_async_remote_copy(
+            src_ref=src,
+            dst_ref=dst,
+            send_sem=hs.at[sem],
+            recv_sem=hr.at[sem],
+            device_id=dev,
+            device_id_type=MESH,
+        )
+
+    to_next = halo_copy(FR.at[pl.ds(rows - HALO, HALO), :], HB.at[0], 0, pn)
+    to_before = halo_copy(FR.at[pl.ds(0, HALO), :], HB.at[1], 1, pb)
+
+    first_sends(0)
+    load_fr.wait()
+    to_next.start()
+    to_before.start()
+    load_out.wait()
+    first_sends(1)
+
+    for ch in range(chunks):
+        TP[ch, 0:KER, :] = taps[:, ch * LANES : (ch + 1) * LANES].astype(jnp.float32)
+
+    def norm_rows(block):
+        values = block.astype(jnp.float32)
+        average = jnp.mean(values, axis=1, keepdims=True)
+        centered = values - average
+        spread_ = jnp.mean(centered * centered, axis=1, keepdims=True)
+        return (centered * lax.rsqrt(spread_ + epsilon) * gain1[...]).astype(jnp.bfloat16)
+
+    step_rows = 32
+
+    def norm_step(i, carry):
+        first = pl.multiple_of(i * step_rows, step_rows)
+        NM[pl.ds(pl.multiple_of(first + HALO, HALO), step_rows), :] = norm_rows(
+            FR[pl.ds(first, step_rows), :]
+        )
+        return carry
+
+    lax.fori_loop(0, rows // step_rows, norm_step, 0)
+
+    first_block = index * nblk
+    last_block = total * nblk - 1
+
+    def block_info(b):
+        u = utts[b]
+        return u, lens[u] - offs[b] * BLK
+
+    info = [
+        block_info(jnp.clip(first_block + i, 0, last_block)) for i in range(-1, nblk + 1)
+    ]
+    joined = []
+    for i in range(nblk + 1):
+        same = info[i][0] == info[i + 1][0]
+        if i == 0:
+            same = same & (first_block > 0)
+        if i == nblk:
+            same = same & (first_block + nblk <= last_block)
+        joined.append(same.astype(jnp.float32))
+    alive_rows = [info[i + 1][1] for i in range(nblk)]
+
+    def tall(count, start):
+        return start + lax.broadcasted_iota(jnp.int32, (count, LANES), 0)
+
+    def project(g):
+        def chunk_step(h, carry):
+            weights = WI[g, :, pl.ds(pl.multiple_of(h * 2 * LANES, 2 * LANES), 2 * LANES)]
+            p = jnp.dot(NM[...], weights, preferred_element_type=jnp.float32)
+            units = p[:, :LANES] * jax.nn.sigmoid(p[:, LANES:])
+            pieces = [
+                jnp.where(tall(HALO, BLK - HALO) < info[0][1], units[:HALO], 0.0)
+            ]
+            for i in range(nblk):
+                part = units[HALO + i * BLK : HALO + (i + 1) * BLK]
+                pieces.append(jnp.where(tall(BLK, 0) < alive_rows[i], part, 0.0))
+            pieces.append(
+                jnp.where(tall(HALO, 0) < info[nblk + 1][1], units[HALO + rows :], 0.0)
+            )
+            pieces = [q.astype(jnp.bfloat16).astype(jnp.float32) for q in pieces]
+            stride = BLK + 2 * HALO
+            for i in range(nblk):
+                base = i * stride
+                GB[base : base + HALO, :] = pieces[i][-HALO:] * joined[i]
+                GB[base + HALO : base + HALO + BLK, :] = pieces[i + 1]
+                GB[base + HALO + BLK : base + stride, :] = pieces[i + 2][:HALO] * joined[i + 1]
+            ch = g * per_group + h
+            tap = [jnp.broadcast_to(TP[ch, k : k + 1, :], (8, LANES)) for k in range(KER)]
+            deep = 4
+            per_block = BLK // (8 * deep)
+
+            def conv_step(j, inner):
+                i, q = j // per_block, j % per_block
+                base = pl.multiple_of(i * stride + q * (8 * deep), 8)
+                sums = [None] * deep
+                for o in range(8 * (deep - 1) + KER):
+                    value = GB[pl.ds(base + (1 + o), 8), :]
+                    for t in range(deep):
+                        k = o - 8 * t
+                        if 0 <= k < KER:
+                            term = value * tap[k]
+                            sums[t] = term if sums[t] is None else sums[t] + term
+                first = pl.multiple_of(j * (8 * deep), 8 * deep)
+                for t in range(deep):
+                    MX[ch, pl.ds(pl.multiple_of(first + 8 * t, 8), 8), :] = sums[t]
+                return inner
+
+            lax.fori_loop(0, nblk * per_block, conv_step, 0)
+            return carry
+
+        lax.fori_loop(0, per_group, chunk_step, 0)
+
+    line(0, 1)
+    at_distance(square_at, 0, 0)
+    line(1, 1)
+    for d in range(2, nz):
+        line(0, d)
+        at_distance(square_at, 0, d - 1)
+        line(1, d)
+        at_distance(square_at, 1, d - 2)
+    to_before.wait_recv()
+    to_next.wait_recv()
+    NM[0:HALO, :] = norm_rows(HB[0])
+    NM[HALO + rows :, :] = norm_rows(HB[1])
+    at_distance(square_at, 0, nz - 1)
+    at_distance(square_at, 1, nz - 2)
+    project(grp)
+    at_distance(corner_at, 0, 0)
+    at_distance(square_at, 1, nz - 1)
+    partner_near(0)
+    project(x * 2 + 1 - c)
+    for d in range(1, nz):
+        at_distance(corner_at, 0, d)
+    at_distance(corner_at, 1, 0)
+    project((1 - x) * 2 + c)
+    partner_far(0)
+    for d in range(1, nz - 1):
+        at_distance(corner_at, 1, d)
+    project((1 - x) * 2 + 1 - c)
+
+    at_distance(corner_at, 1, nz - 1)
+
+    def finish_step(j, carry):
+        first = pl.multiple_of(j * step_rows, step_rows)
+        parts = [MX[ch, pl.ds(first, step_rows), :] for ch in range(chunks)]
+        s1 = parts[0]
+        s2 = parts[0] * parts[0]
+        for part in parts[1:]:
+            s1 = s1 + part
+            s2 = s2 + part * part
+        average = jnp.sum(s1, axis=1, keepdims=True) / float(width)
+        spread_ = jnp.sum(s2, axis=1, keepdims=True) / float(width) - average * average
+        scale = lax.rsqrt(spread_ + epsilon)
+        for ch in range(chunks):
+            cols = slice(ch * LANES, (ch + 1) * LANES)
+            v = (parts[ch] - average) * scale * gain2[:, cols] + bias2[:, cols]
+            ACT[pl.ds(first, step_rows), cols] = (v * jax.nn.sigmoid(v)).astype(jnp.bfloat16)
+        return carry
+
+    lax.fori_loop(0, rows // step_rows, finish_step, 0)
+
+    partner_near(1)
+    partner_far(1)
+
+    wide = 2 * LANES
+
+    def out_copy(n):
+        cols = pl.ds(pl.multiple_of(n * wide, wide), wide)
+        return pltpu.make_async_copy(OUT.at[:, cols], out_hbm.at[:, cols], osem.at[n])
+
+    def out_step(n, carry):
+        cols = pl.ds(pl.multiple_of(n * wide, wide), wide)
+        o = jnp.dot(ACT[...], WO[:, cols], preferred_element_type=jnp.float32)
+        for i in range(nblk):
+            band = slice(i * BLK, (i + 1) * BLK)
+            lived = (
+                lax.broadcasted_iota(jnp.int32, (BLK, wide), 0) < alive_rows[i]
+            ).astype(jnp.float32)
+            OUT[band, cols] = (
+                FR[band, cols].astype(jnp.float32) + o[band] * lived
+            ).astype(jnp.bfloat16)
+        out_copy(n).start()
+        return carry
+
+    lax.fori_loop(0, width // wide, out_step, 0)
+
+    to_next.wait_send()
+    to_before.wait_send()
+    for w in range(2):
+        full = slot(w, x, y, z, c)
+        part = slot(w, x, y, z, c, 0)
+        for d in range(1, nz):
+
+            @pl.when((z >= d - 1) & has_up)
+            def _():
+                copy(w, full, ZU + d - 1, up).wait_send()
+
+            @pl.when((z + d - 1 < nz) & has_down)
+            def _():
+                copy(w, full, ZD + d - 1, down).wait_send()
+
+        for sz in range(nz):
+            copy(w, full, XD + sz, px).wait_send()
+            copy(w, full, YD + sz, py).wait_send()
+            copy(w, part, XH + sz, px).wait_send()
+            copy(w, part, YH + sz, py).wait_send()
+            copy(w, full, PO + sz, pp).wait_send()
+            copy(w, full, PY + sz, pp).wait_send()
+            copy(w, full, PX + sz, pp).wait_send()
+            copy(w, part, PXH + sz, pp).wait_send()
+            copy(w, part, PYH + sz, pp).wait_send()
+    for n in range(width // wide):
+        out_copy(n).wait()
+
+
+def fused_device(
+    frames, ln1_gain, w_in, w_dw, ln2_gain, ln2_bias, w_out, block_utt, block_off, lengths
+):
+    rows, width = frames.shape
+    nz = lax.axis_size("seq") // 2
+    krows, _, cols = w_in.shape
+    groups = cols // LANES
+    wi = w_in.reshape(krows, 2, groups, LANES).transpose(0, 2, 1, 3).reshape(krows, 2 * cols)
+    vmem = pl.BlockSpec(memory_space=pltpu.VMEM)
+    smem = pl.BlockSpec(memory_space=pltpu.SMEM)
+    anywhere = pl.BlockSpec(memory_space=pl.ANY)
+    nsem = 11 * nz - 2
+    nblk = rows // BLK
+    return pl.pallas_call(
+        functools.partial(fused_kernel, nz),
+        out_shape=jax.ShapeDtypeStruct((rows, width), jnp.bfloat16),
+        in_specs=[anywhere] * 3 + [vmem] * 4 + [smem] * 3,
+        out_specs=anywhere,
+        scratch_shapes=[
+            pltpu.VMEM((width // cols, width, 2 * cols), jnp.bfloat16),
+            pltpu.VMEM((width, width), jnp.bfloat16),
+            pltpu.VMEM((rows, width), jnp.bfloat16),
+            pltpu.VMEM((2, HALO, width), jnp.bfloat16),
+            pltpu.VMEM((rows + 2 * HALO, width), jnp.bfloat16),
+            pltpu.VMEM((nblk * (BLK + 2 * HALO), LANES), jnp.float32),
+            pltpu.VMEM((width // LANES, rows, LANES), jnp.float32),
+            pltpu.VMEM((width // LANES, 32, LANES), jnp.float32),
+            pltpu.VMEM((rows, width), jnp.bfloat16),
+            pltpu.VMEM((rows, width), jnp.bfloat16),
+            pltpu.SemaphoreType.DMA((2, nsem)),
+            pltpu.SemaphoreType.DMA((2, nsem)),
+            pltpu.SemaphoreType.DMA((2,)),
+            pltpu.SemaphoreType.DMA((2,)),
+            pltpu.SemaphoreType.DMA((3,)),
+            pltpu.SemaphoreType.DMA((width // (2 * LANES),)),
+        ],
+        compiler_params=pltpu.CompilerParams(
+            collective_id=0, has_side_effects=True, vmem_limit_bytes=40 << 20
+        ),
+    )(
+        frames,
+        wi,
+        w_out,
+        ln1_gain[None],
+        w_dw,
+        ln2_gain[None],
+        ln2_bias[None],
+        block_utt,
+        block_off,
+        lengths,
+    )
+
+
 def solution(mesh):
+    seq, grp = mesh.shape["seq"], mesh.shape["grp"]
+    fits = grp == 4 and seq % 2 == 0 and 4 <= seq <= 8 and D % (seq * LANES) == 0
+
     return jax.shard_map(
-        per_device,
+        fused_device if fits else per_device,
         mesh=mesh,
         in_specs=(
             P(("seq", "grp"), None),

time: 153 us -> 47.6 us (0.31)
  waiting for transfers between devices: 55.8 us -> 0 us
  Pallas kernels: 0 us -> 44.1 us
  other arithmetic: 41.3 us -> 0 us
  blocking collectives: 17 us -> 0 us
  between operations: 13.6 us -> 0.11 us
  local copies, waits for them, and re-layouts: 15.2 us -> 3.3 us
  matrix products: 6.55 us -> 0 us
  starting transfers between devices: 2.81 us -> 0 us
    all_gather x2 -> x0, waiting for transfers between devices: 52.5 us -> none  [the longest x1 33.8 us: per_device(): lax.all_gather(w_in_rows, 'seq', axis=0, tiled=True)]
    pallas_call x0 -> x1, Pallas kernels: none -> 44.1 us  [fused_device(): pl.pallas_call(functools.partial(fused_kernel, nz), out_shape=jax.ShapeDt...]
    select_n x2 -> x0, other arithmetic: 20.2 us -> none  [the longest x1 20.1 us: frame_keys(): return (jnp.where(living, utterance, -1), living[margin:margin + row_count])]
    reduce_sum x3 -> x0, other arithmetic: 20 us -> none  [the longest x1 19.4 us: per_device(): jnp.sum(mixed, axis=1)]
    all_gather x2 -> x0, blocking collectives: 17 us -> none  [the longest x1 10.5 us: per_device(): lax.all_gather(w_in, 'grp', axis=2, tiled=True)]
    gather x4 -> x0, local copies, waits for them, and re-layouts: 11.5 us -> none  [the longest x2 3.9 us: frame_keys(): living = inside & (position < jnp.take(lengths, utterance))]
    dot_general x2 -> x0, matrix products: 6.55 us -> none  [the longest x1 4.06 us: per_device(): jnp.dot(act, lax.all_gather(w_out_rows, 'seq', axis=1, tiled=True), prefe...]
    ppermute x2 -> x0, waiting for transfers between devices: 3.3 us -> none  [the longest x1 3.3 us: extended(): lax.ppermute(lax.slice_in_dim(block, 0, width, axis=dim), axis, backward)]
  transfers between devices with their start and end apart: 4 -> 0, of which waited for: 3 -> 0; matrix products, arithmetic and copies ran while one was open for 39% -> 0% of each run, Pallas kernels for 0% -> 0%
where the time goes in v1:
time: 47.6 us; the launch traced here: 47.5 us
  Pallas kernels  44.1 us (93%)
  local copies, waits for them, and re-layouts  3.3 us (7%)
    pallas_call x1, Pallas kernels, fused_device(): pl.pallas_call(functools.partial(fused_kernel, nz), out_shape=jax.ShapeDt...  44.1 us
    unnamed x19, local copies, waits for them, and re-layouts  2.22 us
    reshape x1, local copies, waits for them, and re-layouts, fused_device(): w_in.reshape(krows, 2, groups, LANES).transpose(0, 2, 1, 3)  1.07 us

profile of v1, /device:TPU:0, one launch (start us, length us, event | category | flops | bytes accessed | tf_op | source)
XLA Modules:
  0.0 47.5 jit_solution(6530234766531159472)
XLA Ops:
  0.0 0.0 copy-start.1
  0.0 0.0 copy-start.2
  0.0 0.0 copy-start.3
  0.0 0.0 copy-start.4
  0.0 0.0 copy-start.5
  0.0 0.0 copy-start.6
  0.0 0.0 copy-start.7
  0.0 0.0 copy-start.8
  0.0 1.1 %reshape.7.wi_hbm = bf16[128,512]{1,0:T(8,128)(2,1)S(1)} reshape(bf16[128,2,2,128]{3,2,1,0:T(2,128)(2,1)} %bitcast.9) | data formatting | bytes 262144 | tf_op jit(solution)/shard_map/reshape | solution.py:538
  1.1 0.0 copy-done.1
  1.1 0.0 copy-done.2
  1.1 0.0 copy-done.3
  1.2 0.0 copy-done.4
  1.2 0.0 copy-done.5
  1.2 0.0 copy-done.6
  1.2 0.0 copy-done.7
  1.2 0.0 copy-done.8
  1.2 0.0 copy-start
  1.2 1.2 %copy-done = bf16[512,1024]{1,0:T(8,128)(2,1)S(1)} copy-done((bf16[512,1024]{1,0:T(8,128)(2,1)S(1)}, bf16[512,1024]{1,0:T(8,128)(2,1)}, u32[]{:S(2)}) %copy-start) | copy-done | bytes 1048600
  2.4 44.1 %shard_map.100 = bf16[512,1024]{1,0:T(8,128)(2,1)S(1)} custom-call(bf16[512,1024]{1,0:T(8,128)(2,1)S(1)} %copy-done, bf16[128,512]{1,0:T(8,128)(2,1)S(1)} %reshape.7.wi_hbm, bf16[256,128]{1,0:T(8,128)(2,1)S(1)} %copy-done.1, f32[1,1024]{1,0:T(1,128)S(1)} %bitcast.6, bf16[31,1024]{1,0:T(8,128)(2,1)S(1)} %copy-done.2, f32[1,1024]{1,0:T(1,128)S(1)} %bitcast.7, ...), custom_call_target="tpu_custom_call" | custom-call | tf_op jit(solution)/shard_map/pallas_call | solution.py:544
  46.5 1.0 %copy.13 = bf16[512,1024]{1,0:T(8,128)(2,1)} copy(bf16[512,1024]{1,0:T(8,128)(2,1)S(1)} %shard_map.100) | data formatting | bytes 2097152
Async XLA Ops:
  0.0 1.1 %copy-start.1 = (bf16[256,128]{1,0:T(8,128)(2,1)S(1)}, bf16[256,128]{1,0:T(8,128)(2,1)}, u32[]{:S(2)}) copy-start(bf16[256,128]{1,0:T(8,128)(2,1)} %wo_hbm.1) | copy-start | bytes 196612
  0.0 1.1 %copy-start.2 = (bf16[31,1024]{1,0:T(8,128)(2,1)S(1)}, bf16[31,1024]{1,0:T(8,128)(2,1)}, u32[]{:S(2)}) copy-start(bf16[31,1024]{1,0:T(8,128)(2,1)} %taps.1) | copy-start | bytes 190468
  0.0 1.1 %copy-start.3 = (f32[1024]{0:T(1024)S(1)}, f32[1024]{0:T(1024)}, u32[]{:S(2)}) copy-start(f32[1024]{0:T(1024)} %param.11) | copy-start | bytes 12292
  0.0 1.1 %copy-start.4 = (f32[1024]{0:T(1024)S(1)}, f32[1024]{0:T(1024)}, u32[]{:S(2)}) copy-start(f32[1024]{0:T(1024)} %param.14) | copy-start | bytes 12292
  0.0 1.2 %copy-start.5 = (f32[1024]{0:T(1024)S(1)}, f32[1024]{0:T(1024)}, u32[]{:S(2)}) copy-start(f32[1024]{0:T(1024)} %param.15) | copy-start | bytes 12292
  0.0 1.2 %copy-start.6 = (s32[128]{0:T(128)S(1)}, s32[128]{0:T(128)}, u32[]{:S(2)}) copy-start(s32[128]{0:T(128)} %utts.1) | copy-start | bytes 1540
  0.0 1.2 %copy-start.7 = (s32[128]{0:T(128)S(1)}, s32[128]{0:T(128)}, u32[]{:S(2)}) copy-start(s32[128]{0:T(128)} %offs.1) | copy-start | bytes 1540
  0.0 1.2 %copy-start.8 = (s32[32]{0:T(128)S(1)}, s32[32]{0:T(128)}, u32[]{:S(2)}) copy-start(s32[32]{0:T(128)} %lens.1) | copy-start | bytes 388
  1.2 1.2 %copy-start = (bf16[512,1024]{1,0:T(8,128)(2,1)S(1)}, bf16[512,1024]{1,0:T(8,128)(2,1)}, u32[]{:S(2)}) copy-start(bf16[512,1024]{1,0:T(8,128)(2,1)} %frames_hbm.1) | copy-start | bytes 3145732

commit v2 on v1

--- a/solution.py
+++ b/solution.py
@@ -382,7 +382,8 @@
         def chunk_step(h, carry):
             weights = WI[g, :, pl.ds(pl.multiple_of(h * 2 * LANES, 2 * LANES), 2 * LANES)]
             p = jnp.dot(NM[...], weights, preferred_element_type=jnp.float32)
-            units = p[:, :LANES] * jax.nn.sigmoid(p[:, LANES:])
+            half = 0.5 * p[:, :LANES]
+            units = half + half * jnp.tanh(0.5 * p[:, LANES:])
             pieces = [
                 jnp.where(tall(HALO, BLK - HALO) < info[0][1], units[:HALO], 0.0)
             ]
@@ -420,7 +421,7 @@
                     MX[ch, pl.ds(pl.multiple_of(first + 8 * t, 8), 8), :] = sums[t]
                 return inner
 
-            lax.fori_loop(0, nblk * per_block, conv_step, 0)
+            lax.fori_loop(0, nblk * per_block, conv_step, 0, unroll=2)
             return carry
 
         lax.fori_loop(0, per_group, chunk_step, 0)
@@ -469,7 +470,8 @@
         for ch in range(chunks):
             cols = slice(ch * LANES, (ch + 1) * LANES)
             v = (parts[ch] - average) * scale * gain2[:, cols] + bias2[:, cols]
-            ACT[pl.ds(first, step_rows), cols] = (v * jax.nn.sigmoid(v)).astype(jnp.bfloat16)
+            v = 0.5 * v
+            ACT[pl.ds(first, step_rows), cols] = (v + v * jnp.tanh(v)).astype(jnp.bfloat16)
         return carry
 
     lax.fori_loop(0, rows // step_rows, finish_step, 0)
@@ -491,10 +493,9 @@
             lived = (
                 lax.broadcasted_iota(jnp.int32, (BLK, wide), 0) < alive_rows[i]
             ).astype(jnp.float32)
-            OUT[band, cols] = (
+            out_hbm[band, cols] = (
                 FR[band, cols].astype(jnp.float32) + o[band] * lived
             ).astype(jnp.bfloat16)
-        out_copy(n).start()
         return carry
 
     lax.fori_loop(0, width // wide, out_step, 0)
@@ -524,8 +525,6 @@
             copy(w, full, PX + sz, pp).wait_send()
             copy(w, part, PXH + sz, pp).wait_send()
             copy(w, part, PYH + sz, pp).wait_send()
-    for n in range(width // wide):
-        out_copy(n).wait()
 
 
 def fused_device(
@@ -545,7 +544,7 @@
         functools.partial(fused_kernel, nz),
         out_shape=jax.ShapeDtypeStruct((rows, width), jnp.bfloat16),
         in_specs=[anywhere] * 3 + [vmem] * 4 + [smem] * 3,
-        out_specs=anywhere,
+        out_specs=vmem,
         scratch_shapes=[
             pltpu.VMEM((width // cols, width, 2 * cols), jnp.bfloat16),
             pltpu.VMEM((width, width), jnp.bfloat16),

time: 47.6 us -> 46.9 us (0.985)
  Pallas kernels: 44.1 us -> 43.3 us
    pallas_call x1, Pallas kernels: 44.1 us -> 43.3 us  [fused_device(): pl.pallas_call(functools.partial(fused_kernel, nz), out_shape=jax.ShapeDt...]
where the time goes in v2:
time: 46.9 us; the launch traced here: 46.8 us
  Pallas kernels  43.3 us (92%)
  local copies, waits for them, and re-layouts  3.3 us (7%)
    pallas_call x1, Pallas kernels, fused_device(): pl.pallas_call(functools.partial(fused_kernel, nz), out_shape=jax.ShapeDt...  43.3 us
    unnamed x19, local copies, waits for them, and re-layouts  2.22 us
    reshape x1, local copies, waits for them, and re-layouts, fused_device(): w_in.reshape(krows, 2, groups, LANES).transpose(0, 2, 1, 3)  1.07 us

profile of v2, /device:TPU:0, one launch (start us, length us, event | category | flops | bytes accessed | tf_op | source)
XLA Modules:
  0.0 46.8 jit_solution(160468280698549806)
XLA Ops:
  0.0 0.0 copy-start.1
  0.0 0.0 copy-start.2
  0.0 0.0 copy-start.3
  0.0 0.0 copy-start.4
  0.0 0.0 copy-start.5
  0.0 0.0 copy-start.6
  0.0 0.0 copy-start.7
  0.0 0.0 copy-start.8
  0.0 1.1 %reshape.7.wi_hbm = bf16[128,512]{1,0:T(8,128)(2,1)S(1)} reshape(bf16[128,2,2,128]{3,2,1,0:T(2,128)(2,1)} %bitcast.9) | data formatting | bytes 262144 | tf_op jit(solution)/shard_map/reshape | solution.py:537
  1.1 0.0 copy-done.1
  1.1 0.0 copy-done.2
  1.1 0.0 copy-done.3
  1.2 0.0 copy-done.4
  1.2 0.0 copy-done.5
  1.2 0.0 copy-done.6
  1.2 0.0 copy-done.7
  1.2 0.0 copy-done.8
  1.2 0.0 copy-start
  1.2 1.2 %copy-done = bf16[512,1024]{1,0:T(8,128)(2,1)S(1)} copy-done((bf16[512,1024]{1,0:T(8,128)(2,1)S(1)}, bf16[512,1024]{1,0:T(8,128)(2,1)}, u32[]{:S(2)}) %copy-start) | copy-done | bytes 1048600
  2.4 43.3 %shard_map.100 = bf16[512,1024]{1,0:T(8,128)(2,1)S(1)} custom-call(bf16[512,1024]{1,0:T(8,128)(2,1)S(1)} %copy-done, bf16[128,512]{1,0:T(8,128)(2,1)S(1)} %reshape.7.wi_hbm, bf16[256,128]{1,0:T(8,128)(2,1)S(1)} %copy-done.1, f32[1,1024]{1,0:T(1,128)S(1)} %bitcast.6, bf16[31,1024]{1,0:T(8,128)(2,1)S(1)} %copy-done.2, f32[1,1024]{1,0:T(1,128)S(1)} %bitcast.7, ...), custom_call_target="tpu_custom_call" | custom-call | tf_op jit(solution)/shard_map/pallas_call | solution.py:543
  45.8 1.0 %copy.13 = bf16[512,1024]{1,0:T(8,128)(2,1)} copy(bf16[512,1024]{1,0:T(8,128)(2,1)S(1)} %shard_map.100) | data formatting | bytes 2097152
Async XLA Ops:
  0.0 1.1 %copy-start.1 = (bf16[256,128]{1,0:T(8,128)(2,1)S(1)}, bf16[256,128]{1,0:T(8,128)(2,1)}, u32[]{:S(2)}) copy-start(bf16[256,128]{1,0:T(8,128)(2,1)} %wo_hbm.1) | copy-start | bytes 196612
  0.0 1.1 %copy-start.2 = (bf16[31,1024]{1,0:T(8,128)(2,1)S(1)}, bf16[31,1024]{1,0:T(8,128)(2,1)}, u32[]{:S(2)}) copy-start(bf16[31,1024]{1,0:T(8,128)(2,1)} %taps.1) | copy-start | bytes 190468
  0.0 1.1 %copy-start.3 = (f32[1024]{0:T(1024)S(1)}, f32[1024]{0:T(1024)}, u32[]{:S(2)}) copy-start(f32[1024]{0:T(1024)} %param.11) | copy-start | bytes 12292
  0.0 1.1 %copy-start.4 = (f32[1024]{0:T(1024)S(1)}, f32[1024]{0:T(1024)}, u32[]{:S(2)}) copy-start(f32[1024]{0:T(1024)} %param.14) | copy-start | bytes 12292
  0.0 1.2 %copy-start.5 = (f32[1024]{0:T(1024)S(1)}, f32[1024]{0:T(1024)}, u32[]{:S(2)}) copy-start(f32[1024]{0:T(1024)} %param.15) | copy-start | bytes 12292
  0.0 1.2 %copy-start.6 = (s32[128]{0:T(128)S(1)}, s32[128]{0:T(128)}, u32[]{:S(2)}) copy-start(s32[128]{0:T(128)} %utts.1) | copy-start | bytes 1540
  0.0 1.2 %copy-start.7 = (s32[128]{0:T(128)S(1)}, s32[128]{0:T(128)}, u32[]{:S(2)}) copy-start(s32[128]{0:T(128)} %offs.1) | copy-start | bytes 1540
  0.0 1.2 %copy-start.8 = (s32[32]{0:T(128)S(1)}, s32[32]{0:T(128)}, u32[]{:S(2)}) copy-start(s32[32]{0:T(128)} %lens.1) | copy-start | bytes 388
  1.2 1.2 %copy-start = (bf16[512,1024]{1,0:T(8,128)(2,1)S(1)}, bf16[512,1024]{1,0:T(8,128)(2,1)}, u32[]{:S(2)}) copy-start(bf16[512,1024]{1,0:T(8,128)(2,1)} %frames_hbm.1) | copy-start | bytes 3145732
